TPU v7x, 512 devices: a whole 4x4x16 slice. The times are simulated.
512 devices in a mesh: gx: 8 (over y, core), gy: 16 (over z), gz: 4 (over x).
Axes of the slice: x: 4, y: 4, z: 16, core: 2. Of those that a mesh axis runs over, the one named last changes fastest.
Arguments:
- source_term: float32 [32, 32, 128, 512], P(None, 'gx', 'gy', 'gz'), may hold values from -16 to 16
- labels: int32 [32, 128, 512], P('gx', 'gy', 'gz'), may hold values from 0 to 5
- conductivity_table: float32 [6], replicated, may hold values from 0.05 to 1
- send_map: int32 [8, 16, 4, 256], P('gx', 'gy', 'gz'), may hold values from -1 to 4095, as said below
- owner_slots: int32 [65536], P(('gx', 'gy', 'gz')), may hold values from 0 to 255, as said below
- sensor_data: float32 [32, 128], replicated, may hold values from -6 to 6
Outputs:
- projections: float32 [3, 128, 65536], P(None, None, ('gx', 'gy', 'gz'))
- gram_blocks: float32 [6, 65536], P(None, ('gx', 'gy', 'gz'))
Inputs may be any that keep to these rules, and one draw needn't show every extreme that they name: `send_map`: entries q * 2 to q * 2 + 1 of row (sx, sy, iz) hold, in their first slots, the brick-local voxels (i * 8 + j) * 128 + k of the positions that this brick sends to owner q = ix * 16 + iy of the same iz, and -1 in the others; no voxel appears twice in a row; some brick fills all 2 slots of some owner. `owner_slots`: the 128 entries of owner d = (ix * 16 + iy) * 4 + iz name, each once, exactly the slots src * 2 + slot that the bricks src = sx * 16 + sy with the same iz fill for it.
All inputs are finite; a program needn't handle non-finite values.
Results may differ from a plain program's by a relative error of at most 0.00012.
Values sent between devices are 32-bit elements; how exact they have to be, the bound alone decides.
A program may use at most 64 MiB of HBM per device.

v0:
```python
import jax
import jax.numpy as jnp
from jax import lax
from jax.sharding import Mesh
from jax.sharding import PartitionSpec as P

GX_GY_GZ = ("gx_0", "gx_1", "gy", "gz")
GX = ("gx_0", "gx_1")
GX_GY = ("gx_0", "gx_1", "gy")
mass_term = 0.25


def extended(block, sides, width):
    for axis, dim in sides:
        count = lax.axis_size(axis)
        forward = [(i, i + 1) for i in range(count - 1)]
        backward = [(target, source) for source, target in forward]
        low = lax.ppermute(
            lax.slice_in_dim(block, block.shape[dim] - width, None, axis=dim), axis, forward
        )
        high = lax.ppermute(lax.slice_in_dim(block, 0, width, axis=dim), axis, backward)
        block = jnp.concatenate([low, block, high], axis=dim)
    return block


def by_axis(x, axes):
    for axis in axes:
        x = lax.psum(x, axis)
    return x


def tissue(shifted, table):
    conductivity = jnp.zeros(shifted.shape, table.dtype)
    for tissue_level in range(table.shape[0]):
        conductivity = conductivity + jnp.where(
            shifted == tissue_level + 1, table[tissue_level], 0.0
        )
    inside = (shifted > 0).astype(table.dtype)
    return (conductivity, inside)


def neighbour_slices(dim_index, offset):
    selection = [slice(1, -1), slice(1, -1), slice(1, -1)]
    selection[dim_index] = slice(2, None) if offset > 0 else slice(0, -2)
    return tuple(selection)


def stencil(padded, conductivity, inside):
    leading = (slice(None),) * (padded.ndim - 3)
    middle = (slice(1, -1), slice(1, -1), slice(1, -1))
    centre = padded[leading + middle]
    own_cond = conductivity[middle]
    own_in = inside[middle]
    accumulated = mass_term * centre
    for dim_index in range(3):
        for offset in (-1, 1):
            beside_all = neighbour_slices(dim_index, offset)
            weight = 0.5 * (own_cond + conductivity[beside_all]) * own_in * inside[beside_all]
            accumulated = accumulated + weight * (centre - padded[leading + beside_all])
    return accumulated


def gram_rows(leadfield):
    entry_pairs = ((0, 0), (1, 1), (2, 2), (0, 1), (0, 2), (1, 2))
    return jnp.stack(
        [jnp.sum(leadfield[first] * leadfield[second], axis=0) for first, second in entry_pairs]
    )


def local_inner(first, second):
    return jnp.sum(first * second, axis=(1, 2, 3))


def per_sensor(values):
    return values[:, None, None, None]


def per_device(source_term, labels, conductivity_table, send_map, owner_slots, sensor_data):
    sensors, size_x, size_y, size_z = source_term.shape
    shifted = labels + 1
    label_pad = extended(shifted, ((GX, 0), ("gy", 1), ("gz", 2)), 2)
    conductivity, inside = tissue(label_pad, conductivity_table)
    source_pad = extended(source_term, ((GX, 1), ("gy", 2), ("gz", 3)), 2)
    applied = stencil(source_pad, conductivity, inside)
    inner_cond = conductivity[1:-1, 1:-1, 1:-1]
    inner_in = inside[1:-1, 1:-1, 1:-1]
    twice_applied = stencil(applied, inner_cond, inner_in)
    applied_core = applied[:, 1:-1, 1:-1, 1:-1]
    moment_zero, moment_one, moment_two, moment_three = (
        by_axis(local_inner(source_term, source_term), GX_GY_GZ),
        by_axis(local_inner(source_term, applied_core), GX_GY_GZ),
        by_axis(local_inner(applied_core, applied_core), GX_GY_GZ),
        by_axis(local_inner(applied_core, twice_applied), GX_GY_GZ),
    )
    first_step = moment_zero / moment_one
    residue = first_step * first_step * moment_two - moment_zero
    growth = 1.0 + residue / moment_zero
    curvature = (
        growth * growth * moment_one
        - 2.0 * growth * first_step * moment_two
        + first_step * first_step * moment_three
    )
    second_step = residue / curvature
    source_coef = first_step + second_step * growth
    applied_coef = second_step * first_step
    solution_pad = (
        per_sensor(source_coef) * source_pad[:, 1:-1, 1:-1, 1:-1]
        - per_sensor(applied_coef) * applied
    )
    cond_inner = conductivity[2:-2, 2:-2, 2:-2]
    voxel_local = jnp.maximum(send_map.reshape(-1), 0)
    index_x = voxel_local // (size_y * size_z)
    index_y = voxel_local // size_z % size_y
    index_z = voxel_local % size_z
    stride_y = size_z + 2
    stride_x = (size_y + 2) * (size_z + 2)
    centre = (index_x + 1) * stride_x + (index_y + 1) * stride_y + (index_z + 1)
    flattened = solution_pad.reshape(sensors, -1)
    cond_here = jnp.take(cond_inner.reshape(-1), voxel_local)

    def gradient(stride):
        upper = jnp.take(flattened, centre + stride, axis=1)
        lower = jnp.take(flattened, centre - stride, axis=1)
        return cond_here * ((upper - lower) * 0.5)

    columns = jnp.stack([gradient(stride_x), gradient(stride_y), gradient(1)])
    received = lax.all_to_all(columns, GX_GY, split_axis=2, concat_axis=2, tiled=True)
    owned = jnp.take(received, owner_slots, axis=2)
    projections = jnp.einsum("csp,st->ctp", owned, sensor_data, precision=lax.Precision.HIGHEST)
    return (projections, gram_rows(owned))


def solution(mesh):
    split = Mesh(
        mesh.devices.reshape(4, 2, mesh.shape["gy"], mesh.shape["gz"]), ("gx_0", "gx_1", "gy", "gz")
    )
    in_specs = (
        P(None, GX, "gy", "gz"),
        P(GX, "gy", "gz"),
        P(),
        P(GX, "gy", "gz", None),
        P(GX_GY_GZ),
        P(),
    )
    out_specs = (P(None, None, GX_GY_GZ), P(None, GX_GY_GZ))
    return jax.shard_map(
        per_device, mesh=split, in_specs=in_specs, out_specs=out_specs, check_vma=False
    )
```

profile of v0, /device:TPU:1, one launch (start us, length us, event | category | flops | bytes accessed | tf_op | source)
XLA Modules:
  0.0 224.1 jit_solution(13874952597590977932)
XLA Ops:
  1.4 4.6 %collective-permute-start.6 = (s32[2,8,128]{2,1,0:T(8,128)S(1)}, s32[2,8,128]{2,1,0:T(8,128)S(1)}, u32[]{:S(2)}, u32[]{:S(2)}) collective-permute-start(s32[2,8,128]{2,1,0:T(8,128)S(1)} %get-tuple-element.70), channel_id=1, source_target_pairs={{0,64},{64,128},{128,192},{192,256},{256,320},{320,384},{384,448},... | collective-permute-start | bytes 24584 | tf_op jit(solution)/shard_map/ppermute | solution.py:18
  6.0 5.5 %collective-permute-start.7 = (s32[2,8,128]{2,1,0:T(8,128)S(1)}, s32[2,8,128]{2,1,0:T(8,128)S(1)}, u32[]{:S(2)}, u32[]{:S(2)}) collective-permute-start(s32[2,8,128]{2,1,0:T(8,128)S(1)} %get-tuple-element.71), channel_id=1, source_target_pairs={{64,0},{128,64},{192,128},{256,192},{320,256},{384,320},{448,384},... | collective-permute-start | bytes 24584 | tf_op jit(solution)/shard_map/ppermute | solution.py:21
  12.5 1.9 collective-permute-start
  14.4 2.4 %collective-permute-start.1 = (f32[32,2,8,128]{3,2,1,0:T(8,128)S(1)}, f32[32,2,8,128]{3,2,1,0:T(8,128)S(1)}, u32[]{:S(2)}, u32[]{:S(2)}) collective-permute-start(f32[32,2,8,128]{3,2,1,0:T(8,128)S(1)} %get-tuple-element.52), channel_id=1, source_target_pairs={{64,0},{128,64},{192,128},{256,192},{320,256},{384,320},{448,384},... | collective-permute-start | bytes 786440 | tf_op jit(solution)/shard_map/ppermute | solution.py:21
  27.2 2.6 %collective-permute-done.9 = s32[8,2,128]{2,1,0:T(2,128)S(1)} collective-permute-done((s32[8,2,128]{2,1,0:T(2,128)S(1)}, s32[8,2,128]{2,1,0:T(2,128)S(1)}, u32[]{:S(2)}, u32[]{:S(2)}) %collective-permute-start.9) | collective-permute-done | bytes 8224 | tf_op jit(solution)/shard_map/ppermute | solution.py:21
  30.0 3.1 %collective-permute-start.10 = (s32[8,12,2]{2,1,0:T(8,128)S(1)}, s32[8,12,2]{2,1,0:T(8,128)S(1)}, u32[]{:S(2)}, u32[]{:S(2)}) collective-permute-start(s32[8,12,2]{2,1,0:T(8,128)S(1)} %get-tuple-element.66), channel_id=1, source_target_pairs={{0,1},{1,2},{2,3},{4,5},{5,6},{6,7},{8,9},{9,10},{10,11},{12,13},{... | collective-permute-start | bytes 2312 | tf_op jit(solution)/shard_map/ppermute | solution.py:18
  35.6 3.3 %collective-permute-done.11 = s32[8,12,2]{2,1,0:T(8,128)S(1)} collective-permute-done((s32[8,12,2]{2,1,0:T(8,128)S(1)}, s32[8,12,2]{2,1,0:T(8,128)S(1)}, u32[]{:S(2)}, u32[]{:S(2)}) %collective-permute-start.11) | collective-permute-done | bytes 800 | tf_op jit(solution)/shard_map/ppermute | solution.py:21
  39.1 3.9 %select_add_fusion = f32[8,12,132]{2,1,0:T(8,128)S(1)} fusion(f32[]{:T(128)} %bitcast.8, f32[]{:T(128)} %bitcast.7, f32[]{:T(128)} %bitcast.6, f32[]{:T(128)} %bitcast.5, f32[]{:T(128)} %bitcast.4, f32[]{:T(128)} %bitcast.3, s32[8,12,2]{2,1,0:T(8,128)S(1)} %collective-permute-done.11, s32[8,2,128]{2,1,0:T(2,128)S(1)} %collective-permute-done.9, ...), kind=kLoop, calls=%fused_computation.79 | loop fusion | flops 291456 | bytes 101400 | tf_op jit(solution)/shard_map/add | solution.py:35
  44.5 3.6 %collective-permute-start.2 = (f32[32,8,2,128]{3,1,2,0:T(8,128)S(1)}, f32[32,8,2,128]{3,1,2,0:T(8,128)S(1)}, u32[]{:S(2)}, u32[]{:S(2)}) collective-permute-start(f32[32,8,2,128]{3,1,2,0:T(8,128)S(1)} %get-tuple-element.49), channel_id=1, source_target_pairs={{0,4},{4,8},{8,12},{12,16},{16,20},{20,24},{24,28},{28,32},{32,36}... | collective-permute-start | bytes 786440 | tf_op jit(solution)/shard_map/ppermute | solution.py:18
  53.1 5.7 %collective-permute-done.3 = f32[32,8,2,128]{3,1,2,0:T(8,128)S(1)} collective-permute-done((f32[32,8,2,128]{3,1,2,0:T(8,128)S(1)}, f32[32,8,2,128]{3,1,2,0:T(8,128)S(1)}, u32[]{:S(2)}, u32[]{:S(2)}) %collective-permute-start.3) | collective-permute-done | bytes 262176 | tf_op jit(solution)/shard_map/ppermute | solution.py:21
  61.6 2.2 copy.93
  66.0 4.2 %collective-permute-start.4 = (f32[32,8,12,2]{0,1,3,2:T(8,128)S(1)}, f32[32,8,12,2]{0,1,3,2:T(8,128)S(1)}, u32[]{:S(2)}, u32[]{:S(2)}) collective-permute-start(f32[32,8,12,2]{0,1,3,2:T(8,128)S(1)} %copy.93), channel_id=1, source_target_pairs={{0,1},{1,2},{2,3},{4,5},{5,6},{6,7},{8,9},{9,10},{10,11},{12,13},{... | collective-permute-start | bytes 73736 | tf_op jit(solution)/shard_map/ppermute | solution.py:18
  76.6 2.4 %copy.95 = f32[32,8,12,2]{3,1,2,0:T(8,128)} copy(f32[32,8,12,2]{0,1,3,2:T(8,128)S(1)} %collective-permute-done.4) | data formatting | bytes 49152 | tf_op jit(solution)/shard_map/ppermute | solution.py:18
  78.9 2.4 %copy.96 = f32[32,8,12,2]{3,1,2,0:T(8,128)} copy(f32[32,8,12,2]{0,1,3,2:T(8,128)S(1)} %collective-permute-done.5) | data formatting | bytes 49152 | tf_op jit(solution)/shard_map/ppermute | solution.py:21
  81.4 4.8 %pad_maximum_fusion = f32[32,8,12,132]{3,1,2,0:T(8,128)S(1)} fusion(f32[32,8,12,2]{3,1,2,0:T(8,128)} %copy.96, f32[32,8,2,128]{3,1,2,0:T(8,128)} %copy-done.11, f32[32,2,8,128]{3,1,2,0:T(2,128)} %copy-done.7, f32[32,4,8,128]{3,1,2,0:T(4,128)} %copy-done.4, f32[32,2,8,128]{3,1,2,0:T(2,128)S(1)} %copy.90, f32[32,8,2,128]{3,1,2,0:T(8,128)} %copy-done.9, ...), kind=kLoop, calls=%fused_computation.8 | loop fusion | flops 2433024 | bytes 3244032 | tf_op jit(solution)/shard_map/concatenate | solution.py:22
  86.3 7.2 %fusion.2 = f32[32,6,10,130]{3,1,2,0:T(8,128)S(1)} fusion(f32[32,8,12,2]{3,1,2,0:T(8,128)S(1)} %copy-done.3, f32[32,8,2,128]{3,1,2,0:T(8,128)S(1)} %copy-done.12, f32[32,8,2,128]{3,1,2,0:T(8,128)S(1)} %copy-done.10, f32[32,2,8,128]{3,1,2,0:T(2,128)S(1)} %copy-done.8, f32[32,4,8,128]{3,1,2,0:T(4,128)S(1)} %copy-done.5, f32[32,2,8,128]{3,1,2,0:T(2,128)S(1)} %copy.90, ...), kind=kLoop, calls=%fused_computation.12 | loop fusion | flops 7238400 | bytes 7799616 | tf_op jit(solution)/shard_map/add | solution.py:59
  95.1 2.4 %multiply_reduce_fusion.1 = (f32[32]{0:T(128)S(1)}, f32[32]{0:T(128)S(1)}, f32[32]{0:T(128)S(1)}) fusion(f32[32,6,10,130]{3,1,2,0:T(8,128)S(1)} %fusion.2, f32[32,4,8,128]{3,2,1,0:T(8,128)S(1)} %copy-done.6, f32[4,8,128]{2,0,1:T(4,128)S(1)} %copy.111, f32[4,8,128]{2,0,1:T(4,128)S(1)} %copy.110, f32[4,8,128]{2,0,1:T(4,128)S(1)} %copy-done.19, ...), kind=kLoop, calls=%fused_computation.60 | loop fusion | flops 3276704 | bytes 4292992 | tf_op jit(solution)/shard_map/reduce_sum | solution.py:71
  97.5 6.0 %all-reduce.2 = (f32[32]{0:T(128)S(1)}, f32[32]{0:T(128)S(1)}, f32[32]{0:T(128)S(1)}, f32[32]{0:T(128)S(1)}) all-reduce(f32[32]{0:T(128)S(1)} %get-tuple-element.15, f32[32]{0:T(128)S(1)} %get-tuple-element.14, f32[32]{0:T(128)S(1)} %copy-done.32, ...), channel_id=1, replica_groups=mesh['gx_0'=4,'gx_1'=2,'gy'=16,'gz'=4] {'gx_0'}, use_global_device_ids=true, to_apply=%region_16.17 | all-reduce | flops 128 | bytes 1024 | tf_op jit(solution)/shard_map/psum | solution.py:28
  103.5 8.6 %all-reduce.3 = (f32[32]{0:T(128)S(1)}, f32[32]{0:T(128)S(1)}, f32[32]{0:T(128)S(1)}, f32[32]{0:T(128)S(1)}) all-reduce(f32[32]{0:T(128)S(1)} %get-tuple-element.33, f32[32]{0:T(128)S(1)} %get-tuple-element.34, f32[32]{0:T(128)S(1)} %get-tuple-element.35, ...), channel_id=1, replica_groups=mesh['gx_0'=4,'gx_1'=2,'gy'=16,'gz'=4] {'gx_1'}, use_global_device_ids=true, to_apply=%region_17.18 | all-reduce | flops 128 | bytes 1024 | tf_op jit(solution)/shard_map/psum | solution.py:28
  112.0 26.8 %all-reduce = (f32[32]{0:T(128)S(1)}, f32[32]{0:T(128)S(1)}, f32[32]{0:T(128)S(1)}, f32[32]{0:T(128)S(1)}) all-reduce(f32[32]{0:T(128)S(1)} %get-tuple-element.37, f32[32]{0:T(128)S(1)} %get-tuple-element.38, f32[32]{0:T(128)S(1)} %get-tuple-element.39, ...), channel_id=1, replica_groups=mesh['gx_0'=4,'gx_1'=2,'gy'=16,'gz'=4] {'gy'}, use_global_device_ids=true, to_apply=%region_18.19 | all-reduce | flops 128 | bytes 1024 | tf_op jit(solution)/shard_map/psum | solution.py:28
  138.9 7.4 %all-reduce.1 = (f32[32]{0:T(128)S(1)}, f32[32]{0:T(128)S(1)}, f32[32]{0:T(128)S(1)}, f32[32]{0:T(128)S(1)}) all-reduce(f32[32]{0:T(128)S(1)} %get-tuple-element.25, f32[32]{0:T(128)S(1)} %get-tuple-element.26, f32[32]{0:T(128)S(1)} %get-tuple-element.27, ...), channel_id=1, replica_groups=mesh['gx_0'=4,'gx_1'=2,'gy'=16,'gz'=4] {'gz'}, use_global_device_ids=true, to_apply=%region_19.20 | all-reduce | flops 128 | bytes 1024 | tf_op jit(solution)/shard_map/psum | solution.py:28
  146.3 4.1 %multiply_subtract_fusion = f32[32,6,10,130]{3,1,2,0:T(8,128)} fusion(f32[32,6,10,130]{3,1,2,0:T(8,128)} %copy-done.1, f32[32,8,12,132]{3,1,2,0:T(8,128)S(1)} %pad_maximum_fusion, f32[32]{0:T(128)S(1)} %mul.415, f32[32]{0:T(128)S(1)} %get-tuple-element.43), kind=kLoop, calls=%fused_computation.37 | loop fusion | flops 748800 | bytes 2995456 | tf_op jit(solution)/shard_map/sub | solution.py:107
  150.5 4.8 %copy.122 = f32[32,6,10,130]{0,3,2,1:T(8,128)} copy(f32[32,6,10,130]{3,1,2,0:T(8,128)} %multiply_subtract_fusion) | data formatting | bytes 1996800 | tf_op jit(solution)/shard_map/reshape | solution.py:118
  155.3 4.8 %reshape.172 = f32[32,7800]{0,1:T(8,128)} reshape(f32[32,6,10,130]{0,3,2,1:T(8,128)} %copy.122) | data formatting | bytes 1996800 | tf_op jit(solution)/shard_map/reshape | solution.py:118
  160.1 3.0 %gather_fusion.7 = f32[256,32]{1,0:T(8,128)S(1)} fusion(f32[32,7800]{0,1:T(8,128)} %reshape.172, s32[1024]{0:T(1024)} %get-tuple-element.96), kind=kCustom, calls=%fused_computation.5.clone | custom fusion | bytes 66560 | tf_op jit(solution)/shard_map/jit(_take)/gather | solution.py:123
  163.0 3.0 %gather_fusion.6 = f32[256,32]{1,0:T(8,128)S(1)} fusion(f32[32,7800]{0,1:T(8,128)} %reshape.172, s32[1024]{0:T(1024)} %get-tuple-element.97), kind=kCustom, calls=%fused_computation.4.clone | custom fusion | bytes 66560 | tf_op jit(solution)/shard_map/jit(_take)/gather | solution.py:122
  166.0 3.0 %gather_fusion.5 = f32[256,32]{1,0:T(8,128)S(1)} fusion(f32[32,7800]{0,1:T(8,128)} %reshape.172, s32[1024]{0:T(1024)} %get-tuple-element.98), kind=kCustom, calls=%fused_computation.3.clone | custom fusion | bytes 66560 | tf_op jit(solution)/shard_map/jit(_take)/gather | solution.py:123
  169.0 3.0 %gather_fusion.4 = f32[256,32]{1,0:T(8,128)S(1)} fusion(f32[32,7800]{0,1:T(8,128)} %reshape.172, s32[1024]{0:T(1024)} %get-tuple-element.99), kind=kCustom, calls=%fused_computation.2.clone | custom fusion | bytes 66560 | tf_op jit(solution)/shard_map/jit(_take)/gather | solution.py:122
  172.0 3.0 %gather_fusion.3 = f32[256,32]{1,0:T(8,128)S(1)} fusion(f32[32,7800]{0,1:T(8,128)} %reshape.172, s32[1024]{0:T(1024)} %get-tuple-element.100), kind=kCustom, calls=%fused_computation.1.clone | custom fusion | bytes 66560 | tf_op jit(solution)/shard_map/jit(_take)/gather | solution.py:123
  175.0 3.0 %gather_fusion.2 = f32[256,32]{1,0:T(8,128)S(1)} fusion(f32[32,7800]{0,1:T(8,128)} %reshape.172, s32[1024]{0:T(1024)} %get-tuple-element.101), kind=kCustom, calls=%fused_computation.clone | custom fusion | bytes 66560 | tf_op jit(solution)/shard_map/jit(_take)/gather | solution.py:122
  179.8 20.1 %all-to-all-start = ((f32[128,1,192]{2,1,0:T(1,128)}), f32[128,1,192]{2,1,0:T(1,128)S(1)}, u32[]{:S(2)}, u32[]{:S(2)}) async-start(f32[128,1,192]{2,1,0:T(1,128)} %reshape.176), calls=%async_computation | async-start | bytes 262144 | tf_op jit(solution)/shard_map/all_to_all | solution.py:127
  199.9 18.2 %all-to-all-done = f32[128,1,192]{2,1,0:T(1,128)S(1)} async-done(((f32[128,1,192]{2,1,0:T(1,128)}), f32[128,1,192]{2,1,0:T(1,128)S(1)}, u32[]{:S(2)}, u32[]{:S(2)}) %all-to-all-start) | async-done | bytes 98336 | tf_op jit(solution)/shard_map/all_to_all | solution.py:127
  (146 shorter events, 42.0 us)
Async XLA Ops:
  0.6 221.8 %copy-start = (f32[32,128]{1,0:T(8,128)S(1)}, f32[32,128]{1,0:T(8,128)}, u32[]{:S(2)}) copy-start(f32[32,128]{1,0:T(8,128)} %param.13) | copy-start | bytes 49156
  1.4 22.6 %collective-permute-start.6 = (s32[2,8,128]{2,1,0:T(8,128)S(1)}, s32[2,8,128]{2,1,0:T(8,128)S(1)}, u32[]{:S(2)}, u32[]{:S(2)}) collective-permute-start(s32[2,8,128]{2,1,0:T(8,128)S(1)} %get-tuple-element.70), channel_id=1, source_target_pairs={{0,64},{64,128},{128,192},{192,256},{256,320},{320,384},{384,448},... | collective-permute-start | bytes 24584 | tf_op jit(solution)/shard_map/ppermute | solution.py:18
  6.0 18.1 %collective-permute-start.7 = (s32[2,8,128]{2,1,0:T(8,128)S(1)}, s32[2,8,128]{2,1,0:T(8,128)S(1)}, u32[]{:S(2)}, u32[]{:S(2)}) collective-permute-start(s32[2,8,128]{2,1,0:T(8,128)S(1)} %get-tuple-element.71), channel_id=1, source_target_pairs={{64,0},{128,64},{192,128},{256,192},{320,256},{384,320},{448,384},... | collective-permute-start | bytes 24584 | tf_op jit(solution)/shard_map/ppermute | solution.py:21
  12.5 31.5 %collective-permute-start = (f32[32,2,8,128]{3,2,1,0:T(8,128)S(1)}, f32[32,2,8,128]{3,2,1,0:T(8,128)S(1)}, u32[]{:S(2)}, u32[]{:S(2)}) collective-permute-start(f32[32,2,8,128]{3,2,1,0:T(8,128)S(1)} %get-tuple-element.51), channel_id=1, source_target_pairs={{0,64},{64,128},{128,192},{192,256},{256,320},{320,384},{384,448},... | collective-permute-start | bytes 786440 | tf_op jit(solution)/shard_map/ppermute | solution.py:18
  14.4 29.7 %collective-permute-start.1 = (f32[32,2,8,128]{3,2,1,0:T(8,128)S(1)}, f32[32,2,8,128]{3,2,1,0:T(8,128)S(1)}, u32[]{:S(2)}, u32[]{:S(2)}) collective-permute-start(f32[32,2,8,128]{3,2,1,0:T(8,128)S(1)} %get-tuple-element.52), channel_id=1, source_target_pairs={{64,0},{128,64},{192,128},{256,192},{320,256},{384,320},{448,384},... | collective-permute-start | bytes 786440 | tf_op jit(solution)/shard_map/ppermute | solution.py:21
  24.0 3.2 %collective-permute-start.8 = (s32[8,2,128]{2,1,0:T(2,128)S(1)}, s32[8,2,128]{2,1,0:T(2,128)S(1)}, u32[]{:S(2)}, u32[]{:S(2)}) collective-permute-start(s32[8,2,128]{2,1,0:T(2,128)S(1)} %get-tuple-element.68), channel_id=1, source_target_pairs={{0,4},{4,8},{8,12},{12,16},{16,20},{20,24},{24,28},{28,32},{32,36}... | collective-permute-start | bytes 24584 | tf_op jit(solution)/shard_map/ppermute | solution.py:18
  25.3 4.5 %collective-permute-start.9 = (s32[8,2,128]{2,1,0:T(2,128)S(1)}, s32[8,2,128]{2,1,0:T(2,128)S(1)}, u32[]{:S(2)}, u32[]{:S(2)}) collective-permute-start(s32[8,2,128]{2,1,0:T(2,128)S(1)} %get-tuple-element.69), channel_id=1, source_target_pairs={{4,0},{8,4},{12,8},{16,12},{20,16},{24,20},{28,24},{32,28},{36,32}... | collective-permute-start | bytes 24584 | tf_op jit(solution)/shard_map/ppermute | solution.py:21
  30.0 5.6 %collective-permute-start.10 = (s32[8,12,2]{2,1,0:T(8,128)S(1)}, s32[8,12,2]{2,1,0:T(8,128)S(1)}, u32[]{:S(2)}, u32[]{:S(2)}) collective-permute-start(s32[8,12,2]{2,1,0:T(8,128)S(1)} %get-tuple-element.66), channel_id=1, source_target_pairs={{0,1},{1,2},{2,3},{4,5},{5,6},{6,7},{8,9},{9,10},{10,11},{12,13},{... | collective-permute-start | bytes 2312 | tf_op jit(solution)/shard_map/ppermute | solution.py:18
  33.1 5.9 %collective-permute-start.11 = (s32[8,12,2]{2,1,0:T(8,128)S(1)}, s32[8,12,2]{2,1,0:T(8,128)S(1)}, u32[]{:S(2)}, u32[]{:S(2)}) collective-permute-start(s32[8,12,2]{2,1,0:T(8,128)S(1)} %get-tuple-element.67), channel_id=1, source_target_pairs={{1,0},{2,1},{3,2},{5,4},{6,5},{7,6},{9,8},{10,9},{11,10},{13,12},{... | collective-permute-start | bytes 2312 | tf_op jit(solution)/shard_map/ppermute | solution.py:21
  35.6 23.3 %copy-start.4 = (f32[32,4,8,128]{3,1,2,0:T(4,128)}, f32[32,4,8,128]{3,1,2,0:T(4,128)S(1)}, u32[]{:S(2)}) copy-start(f32[32,4,8,128]{3,1,2,0:T(4,128)S(1)} %copy.105) | copy-start | bytes 1572868
  44.3 15.6 %copy-start.7 = (f32[32,2,8,128]{3,1,2,0:T(2,128)}, f32[32,2,8,128]{3,1,2,0:T(2,128)S(1)}, u32[]{:S(2)}) copy-start(f32[32,2,8,128]{3,1,2,0:T(2,128)S(1)} %copy.92) | copy-start | bytes 786436
  44.5 8.6 %collective-permute-start.2 = (f32[32,8,2,128]{3,1,2,0:T(8,128)S(1)}, f32[32,8,2,128]{3,1,2,0:T(8,128)S(1)}, u32[]{:S(2)}, u32[]{:S(2)}) collective-permute-start(f32[32,8,2,128]{3,1,2,0:T(8,128)S(1)} %get-tuple-element.49), channel_id=1, source_target_pairs={{0,4},{4,8},{8,12},{12,16},{16,20},{20,24},{24,28},{28,32},{32,36}... | collective-permute-start | bytes 786440 | tf_op jit(solution)/shard_map/ppermute | solution.py:18
  48.0 10.8 %collective-permute-start.3 = (f32[32,8,2,128]{3,1,2,0:T(8,128)S(1)}, f32[32,8,2,128]{3,1,2,0:T(8,128)S(1)}, u32[]{:S(2)}, u32[]{:S(2)}) collective-permute-start(f32[32,8,2,128]{3,1,2,0:T(8,128)S(1)} %get-tuple-element.50), channel_id=1, source_target_pairs={{4,0},{8,4},{12,8},{16,12},{20,16},{24,20},{28,24},{32,28},{36,32}... | collective-permute-start | bytes 786440 | tf_op jit(solution)/shard_map/ppermute | solution.py:21
  61.6 9.1 %copy-start.25 = (f32[4,8,128]{2,1,0:T(8,128)S(1)}, f32[4,8,128]{2,1,0:T(8,128)}, u32[]{:S(2)}) copy-start(f32[4,8,128]{2,1,0:T(8,128)} %get-tuple-element.58) | copy-start | bytes 49156
  61.6 9.1 %copy-start.24 = (f32[4,8,128]{2,1,0:T(8,128)S(1)}, f32[4,8,128]{2,1,0:T(8,128)}, u32[]{:S(2)}) copy-start(f32[4,8,128]{2,1,0:T(8,128)} %get-tuple-element.53) | copy-start | bytes 49156
  61.6 9.7 %copy-start.23 = (f32[4,8,128]{2,1,0:T(8,128)S(1)}, f32[4,8,128]{2,1,0:T(8,128)}, u32[]{:S(2)}) copy-start(f32[4,8,128]{2,1,0:T(8,128)} %get-tuple-element.54) | copy-start | bytes 49156
  61.6 10.3 %copy-start.22 = (f32[4,8,128]{2,1,0:T(8,128)S(1)}, f32[4,8,128]{2,1,0:T(8,128)}, u32[]{:S(2)}) copy-start(f32[4,8,128]{2,1,0:T(8,128)} %get-tuple-element.55) | copy-start | bytes 49156
  64.7 14.2 %collective-permute-start.5 = (f32[32,8,12,2]{0,1,3,2:T(8,128)S(1)}, f32[32,8,12,2]{0,1,3,2:T(8,128)S(1)}, u32[]{:S(2)}, u32[]{:S(2)}) collective-permute-start(f32[32,8,12,2]{0,1,3,2:T(8,128)S(1)} %copy.94), channel_id=1, source_target_pairs={{1,0},{2,1},{3,2},{5,4},{6,5},{7,6},{9,8},{10,9},{11,10},{13,12},{... | collective-permute-start | bytes 73736 | tf_op jit(solution)/shard_map/ppermute | solution.py:21
  66.0 10.5 %collective-permute-start.4 = (f32[32,8,12,2]{0,1,3,2:T(8,128)S(1)}, f32[32,8,12,2]{0,1,3,2:T(8,128)S(1)}, u32[]{:S(2)}, u32[]{:S(2)}) collective-permute-start(f32[32,8,12,2]{0,1,3,2:T(8,128)S(1)} %copy.93), channel_id=1, source_target_pairs={{0,1},{1,2},{2,3},{4,5},{5,6},{6,7},{8,9},{9,10},{10,11},{12,13},{... | collective-permute-start | bytes 73736 | tf_op jit(solution)/shard_map/ppermute | solution.py:18
  86.3 8.8 %copy-start.6 = (f32[32,4,8,128]{3,2,1,0:T(8,128)S(1)}, f32[32,4,8,128]{3,2,1,0:T(8,128)}, u32[]{:S(2)}) copy-start(f32[32,4,8,128]{3,2,1,0:T(8,128)} %param.8) | copy-start | bytes 1572868
  86.3 8.8 %copy-start.18 = (f32[4,8,128]{2,0,1:T(4,128)S(1)}, f32[4,8,128]{2,0,1:T(4,128)}, u32[]{:S(2)}) copy-start(f32[4,8,128]{2,0,1:T(4,128)} %copy.106) | copy-start | bytes 49156
  86.3 8.8 %copy-start.19 = (f32[4,8,128]{2,0,1:T(4,128)S(1)}, f32[4,8,128]{2,0,1:T(4,128)}, u32[]{:S(2)}) copy-start(f32[4,8,128]{2,0,1:T(4,128)} %copy.109) | copy-start | bytes 49156
  86.3 8.8 %copy-start.20 = (f32[4,8,128]{2,0,1:T(4,128)S(1)}, f32[4,8,128]{2,0,1:T(4,128)}, u32[]{:S(2)}) copy-start(f32[4,8,128]{2,0,1:T(4,128)} %copy.108) | copy-start | bytes 49156
  155.2 22.8 %copy-start.26 = (f32[256]{0:T(256)S(1)}, f32[256]{0:T(256)}, u32[]{:S(2)}) copy-start(f32[256]{0:T(256)} %select_multiply_fusion) | copy-start | bytes 3076
  155.2 22.8 %copy-start.27 = (pred[256]{0:T(512)(128)(4,1)S(1)}, pred[256]{0:T(512)(128)(4,1)}, u32[]{:S(2)}) copy-start(pred[256]{0:T(512)(128)(4,1)} %get-tuple-element.75) | copy-start | bytes 772
  155.2 22.8 %copy-start.28 = (pred[256]{0:T(512)(128)(4,1)S(1)}, pred[256]{0:T(512)(128)(4,1)}, u32[]{:S(2)}) copy-start(pred[256]{0:T(512)(128)(4,1)} %get-tuple-element.76) | copy-start | bytes 772
  155.2 22.8 %copy-start.29 = (pred[256]{0:T(512)(128)(4,1)S(1)}, pred[256]{0:T(512)(128)(4,1)}, u32[]{:S(2)}) copy-start(pred[256]{0:T(512)(128)(4,1)} %get-tuple-element.77) | copy-start | bytes 772
  155.3 22.8 %copy-start.30 = (pred[256]{0:T(512)(128)(4,1)S(1)}, pred[256]{0:T(512)(128)(4,1)}, u32[]{:S(2)}) copy-start(pred[256]{0:T(512)(128)(4,1)} %get-tuple-element.78) | copy-start | bytes 772
  155.3 22.8 %copy-start.31 = (pred[256]{0:T(512)(128)(4,1)S(1)}, pred[256]{0:T(512)(128)(4,1)}, u32[]{:S(2)}) copy-start(pred[256]{0:T(512)(128)(4,1)} %get-tuple-element.79) | copy-start | bytes 772
  155.3 22.8 %copy-start.33 = (pred[256]{0:T(512)(128)(4,1)S(1)}, pred[256]{0:T(512)(128)(4,1)}, u32[]{:S(2)}) copy-start(pred[256]{0:T(512)(128)(4,1)} %get-tuple-element.41) | copy-start | bytes 772
  163.0 36.8 %copy-start.34 = (s32[128]{0:T(128)S(1)}, s32[128]{0:T(128)}, u32[]{:S(2)}) copy-start(s32[128]{0:T(128)} %param.12) | copy-start | bytes 1540
  179.8 38.3 %all-to-all-start = ((f32[128,1,192]{2,1,0:T(1,128)}), f32[128,1,192]{2,1,0:T(1,128)S(1)}, u32[]{:S(2)}, u32[]{:S(2)}) async-start(f32[128,1,192]{2,1,0:T(1,128)} %reshape.176), calls=%async_computation | async-start | bytes 262144 | tf_op jit(solution)/shard_map/all_to_all | solution.py:127
  (16 other events, 73.0 us)
where the time goes:
time: 225 us; the launch traced here: 224 us
  local copies, waits for them, and re-layouts  55.3 us (25%)
  starting transfers between devices  51.7 us (23%)
  blocking collectives  48.8 us (22%)
  other arithmetic  35.7 us (16%)
  waiting for transfers between devices  31 us (14%)
    psum x4, blocking collectives, by_axis(): x = lax.psum(x, axis)  48.8 us
    all_to_all x1, starting transfers between devices, per_device(): lax.all_to_all(columns, GX_GY, split_axis=2, concat_axis=2, tiled=True)  20.1 us
    ppermute x6, starting transfers between devices, extended(): lax.ppermute(lax.slice_in_dim(block, block.shape[dim] - width, None, axis...  18.6 us
    all_to_all x1, waiting for transfers between devices, per_device(): lax.all_to_all(columns, GX_GY, split_axis=2, concat_axis=2, tiled=True)  18.2 us
    ppermute x6, starting transfers between devices, extended(): lax.ppermute(lax.slice_in_dim(block, 0, width, axis=dim), axis, backward)  13 us
    ppermute x6, waiting for transfers between devices, extended(): lax.ppermute(lax.slice_in_dim(block, 0, width, axis=dim), axis, backward)  11.7 us
    reshape x2, local copies, waits for them, and re-layouts, per_device(): flattened = solution_pad.reshape(sensors, -1)  9.55 us
    gather x3, local copies, waits for them, and re-layouts, gradient(): upper = jnp.take(flattened, centre + stride, axis=1)  8.98 us
  transfers between devices with their start and end apart: 13, of which 5 were waited for; matrix products, arithmetic and copies ran while one was open for 12% of the time, Pallas kernels for 0%

commit v1 on v0

--- a/solution.py
+++ b/solution.py
@@ -25,7 +25,7 @@
 
 def by_axis(x, axes):
     for axis in axes:
-        x = lax.psum(x, axis)
+        x = jnp.sum(lax.all_gather(x, axis), axis=0)
     return x
 
 

time: 225 us -> 236 us (1.049)
  local copies, waits for them, and re-layouts: 55.3 us -> 66 us
  waiting for transfers between devices: 31 us -> 26.5 us
  between operations: 1.36 us -> 3.91 us
    unnamed x0 -> x4, blocking collectives: none -> 50.4 us
    psum x4 -> x0, blocking collectives: 48.8 us -> none  [by_axis(): x = lax.psum(x, axis)]
    unnamed x74 -> x112, local copies, waits for them, and re-layouts: 5.64 us -> 15 us
    ppermute x6, waiting for transfers between devices: 11.7 us -> 6.34 us  [extended(): lax.ppermute(lax.slice_in_dim(block, 0, width, axis=dim), axis, backward)]
  transfers between devices with their start and end apart: 13 -> 13, of which waited for: 5 -> 4; matrix products, arithmetic and copies ran while one was open for 12% -> 14% of each run, Pallas kernels for 0% -> 0%
where the time goes in v1:
time: 236 us; the launch traced here: 234 us
  local copies, waits for them, and re-layouts  66 us (28%)
  starting transfers between devices  51.6 us (22%)
  blocking collectives  50.4 us (21%)
  other arithmetic  35.6 us (15%)
  waiting for transfers between devices  26.5 us (11%)
  between operations  3.91 us (2%)
    unnamed x4, blocking collectives  50.4 us
    all_to_all x1, starting transfers between devices, per_device(): lax.all_to_all(columns, GX_GY, split_axis=2, concat_axis=2, tiled=True)  19.6 us
    ppermute x6, starting transfers between devices, extended(): lax.ppermute(lax.slice_in_dim(block, block.shape[dim] - width, None, axis...  19 us
    all_to_all x1, waiting for transfers between devices, per_device(): lax.all_to_all(columns, GX_GY, split_axis=2, concat_axis=2, tiled=True)  18.2 us
    unnamed x112, local copies, waits for them, and re-layouts  15 us
    ppermute x6, starting transfers between devices, extended(): lax.ppermute(lax.slice_in_dim(block, 0, width, axis=dim), axis, backward)  13 us
    reshape x2, local copies, waits for them, and re-layouts, per_device(): flattened = solution_pad.reshape(sensors, -1)  9.57 us
    gather x3, local copies, waits for them, and re-layouts, gradient(): upper = jnp.take(flattened, centre + stride, axis=1)  8.98 us
  transfers between devices with their start and end apart: 13, of which 4 were waited for; matrix products, arithmetic and copies ran while one was open for 14% of the time, Pallas kernels for 0%

profile of v1, /device:TPU:1, one launch (start us, length us, event | category | flops | bytes accessed | tf_op | source)
XLA Modules:
  0.0 234.2 jit_solution(8973652074910323684)
XLA Ops:
  1.4 4.6 %collective-permute-start.6 = (s32[2,8,128]{2,1,0:T(8,128)S(1)}, s32[2,8,128]{2,1,0:T(8,128)S(1)}, u32[]{:S(2)}, u32[]{:S(2)}) collective-permute-start(s32[2,8,128]{2,1,0:T(8,128)S(1)} %get-tuple-element.70), channel_id=1, source_target_pairs={{0,64},{64,128},{128,192},{192,256},{256,320},{320,384},{384,448},... | collective-permute-start | bytes 24584 | tf_op jit(solution)/shard_map/ppermute | solution.py:18
  6.0 5.5 %collective-permute-start.7 = (s32[2,8,128]{2,1,0:T(8,128)S(1)}, s32[2,8,128]{2,1,0:T(8,128)S(1)}, u32[]{:S(2)}, u32[]{:S(2)}) collective-permute-start(s32[2,8,128]{2,1,0:T(8,128)S(1)} %get-tuple-element.71), channel_id=1, source_target_pairs={{64,0},{128,64},{192,128},{256,192},{320,256},{384,320},{448,384},... | collective-permute-start | bytes 24584 | tf_op jit(solution)/shard_map/ppermute | solution.py:21
  12.5 1.9 collective-permute-start
  14.4 2.4 %collective-permute-start.1 = (f32[32,2,8,128]{3,2,1,0:T(8,128)S(1)}, f32[32,2,8,128]{3,2,1,0:T(8,128)S(1)}, u32[]{:S(2)}, u32[]{:S(2)}) collective-permute-start(f32[32,2,8,128]{3,2,1,0:T(8,128)S(1)} %get-tuple-element.52), channel_id=1, source_target_pairs={{64,0},{128,64},{192,128},{256,192},{320,256},{384,320},{448,384},... | collective-permute-start | bytes 786440 | tf_op jit(solution)/shard_map/ppermute | solution.py:21
  30.1 3.1 %collective-permute-start.10 = (s32[8,12,2]{2,1,0:T(8,128)S(1)}, s32[8,12,2]{2,1,0:T(8,128)S(1)}, u32[]{:S(2)}, u32[]{:S(2)}) collective-permute-start(s32[8,12,2]{2,1,0:T(8,128)S(1)} %get-tuple-element.66), channel_id=1, source_target_pairs={{0,1},{1,2},{2,3},{4,5},{5,6},{6,7},{8,9},{9,10},{10,11},{12,13},{... | collective-permute-start | bytes 2312 | tf_op jit(solution)/shard_map/ppermute | solution.py:18
  41.8 3.9 %select_add_fusion = f32[8,12,132]{2,1,0:T(8,128)S(1)} fusion(f32[]{:T(128)} %bitcast.12, f32[]{:T(128)} %bitcast.11, f32[]{:T(128)} %bitcast.10, f32[]{:T(128)} %bitcast.9, f32[]{:T(128)} %bitcast.8, f32[]{:T(128)} %bitcast.7, s32[8,12,2]{2,1,0:T(8,128)S(1)} %collective-permute-done.11, s32[8,2,128]{2,1,0:T(2,128)S(1)} %collective-permute-done.9, ...), kind=kLoop, calls=%fused_computation.79 | loop fusion | flops 291456 | bytes 101400 | tf_op jit(solution)/shard_map/add | solution.py:35
  47.1 3.6 %collective-permute-start.2 = (f32[32,8,2,128]{3,1,2,0:T(8,128)S(1)}, f32[32,8,2,128]{3,1,2,0:T(8,128)S(1)}, u32[]{:S(2)}, u32[]{:S(2)}) collective-permute-start(f32[32,8,2,128]{3,1,2,0:T(8,128)S(1)} %get-tuple-element.49), channel_id=1, source_target_pairs={{0,4},{4,8},{8,12},{12,16},{16,20},{20,24},{24,28},{28,32},{32,36}... | collective-permute-start | bytes 786440 | tf_op jit(solution)/shard_map/ppermute | solution.py:18
  52.7 1.7 gather_fusion
  54.7 1.9 collective-permute-done.2
  56.6 5.6 %collective-permute-done.3 = f32[32,8,2,128]{3,1,2,0:T(8,128)S(1)} collective-permute-done((f32[32,8,2,128]{3,1,2,0:T(8,128)S(1)}, f32[32,8,2,128]{3,1,2,0:T(8,128)S(1)}, u32[]{:S(2)}, u32[]{:S(2)}) %collective-permute-start.3) | collective-permute-done | bytes 262176 | tf_op jit(solution)/shard_map/ppermute | solution.py:21
  65.0 2.2 copy.93
  69.4 4.5 %collective-permute-start.4 = (f32[32,8,12,2]{0,1,3,2:T(8,128)S(1)}, f32[32,8,12,2]{0,1,3,2:T(8,128)S(1)}, u32[]{:S(2)}, u32[]{:S(2)}) collective-permute-start(f32[32,8,12,2]{0,1,3,2:T(8,128)S(1)} %copy.93), channel_id=1, source_target_pairs={{0,1},{1,2},{2,3},{4,5},{5,6},{6,7},{8,9},{9,10},{10,11},{12,13},{... | collective-permute-start | bytes 73736 | tf_op jit(solution)/shard_map/ppermute | solution.py:18
  80.4 2.4 %copy.95 = f32[32,8,12,2]{3,1,2,0:T(8,128)} copy(f32[32,8,12,2]{0,1,3,2:T(8,128)S(1)} %collective-permute-done.4) | data formatting | bytes 49152 | tf_op jit(solution)/shard_map/ppermute | solution.py:18
  82.7 2.4 %copy.96 = f32[32,8,12,2]{3,1,2,0:T(8,128)} copy(f32[32,8,12,2]{0,1,3,2:T(8,128)S(1)} %collective-permute-done.5) | data formatting | bytes 49152 | tf_op jit(solution)/shard_map/ppermute | solution.py:21
  85.2 4.8 %pad_maximum_fusion = f32[32,8,12,132]{3,1,2,0:T(8,128)S(1)} fusion(f32[32,8,12,2]{3,1,2,0:T(8,128)} %copy.96, f32[32,8,2,128]{3,1,2,0:T(8,128)} %copy-done.11, f32[32,2,8,128]{3,1,2,0:T(2,128)} %copy-done.7, f32[32,4,8,128]{3,1,2,0:T(4,128)} %copy-done.4, f32[32,2,8,128]{3,1,2,0:T(2,128)S(1)} %copy.90, f32[32,8,2,128]{3,1,2,0:T(8,128)} %copy-done.9, ...), kind=kLoop, calls=%fused_computation.8 | loop fusion | flops 2433024 | bytes 3244032 | tf_op jit(solution)/shard_map/concatenate | solution.py:22
  90.2 7.2 %fusion.2 = f32[32,6,10,130]{3,1,2,0:T(8,128)S(1)} fusion(f32[32,8,12,2]{3,1,2,0:T(8,128)S(1)} %copy-done.3, f32[32,8,2,128]{3,1,2,0:T(8,128)S(1)} %copy-done.12, f32[32,8,2,128]{3,1,2,0:T(8,128)S(1)} %copy-done.10, f32[32,2,8,128]{3,1,2,0:T(2,128)S(1)} %copy-done.8, f32[32,4,8,128]{3,1,2,0:T(4,128)S(1)} %copy-done.5, f32[32,2,8,128]{3,1,2,0:T(2,128)S(1)} %copy.90, ...), kind=kLoop, calls=%fused_computation.12 | loop fusion | flops 7238400 | bytes 7799616 | tf_op jit(solution)/shard_map/add | solution.py:59
  98.9 2.4 %multiply_reduce_fusion.1 = (f32[32]{0:T(128)S(1)}, f32[32]{0:T(128)S(1)}, f32[32]{0:T(128)S(1)}) fusion(f32[32,6,10,130]{3,1,2,0:T(8,128)S(1)} %fusion.2, f32[32,4,8,128]{3,2,1,0:T(8,128)S(1)} %copy-done.6, f32[4,8,128]{2,0,1:T(4,128)S(1)} %copy.111, f32[4,8,128]{2,0,1:T(4,128)S(1)} %copy.110, f32[4,8,128]{2,0,1:T(4,128)S(1)} %copy-done.19, ...), kind=kLoop, calls=%fused_computation.60 | loop fusion | flops 3276704 | bytes 4292992 | tf_op jit(solution)/shard_map/reduce_sum | solution.py:71
  101.9 6.0 %all-reduce.18 = (f32[128]{0:T(128)S(1)}, f32[128]{0:T(128)S(1)}, f32[128]{0:T(128)S(1)}, f32[128]{0:T(128)S(1)}) all-reduce(f32[128]{0:T(128)S(1)} %dynamic-update-slice.12, f32[128]{0:T(128)S(1)} %dynamic-update-slice.8, f32[128]{0:T(128)S(1)} %copy-done.34, ...), channel_id=14, replica_groups=mesh['gx_0'=4,'gx_1'=2,'gy'=16,'gz'=4] {'gx_0'}, use_global_device_ids=true, to_apply=%add.12 | all-reduce | flops 512 | bytes 4096
  109.3 8.0 %all-reduce.19 = (f32[64]{0:T(128)S(1)}, f32[64]{0:T(128)S(1)}, f32[64]{0:T(128)S(1)}, f32[64]{0:T(128)S(1)}) all-reduce(f32[64]{0:T(128)S(1)} %dynamic-update-slice.13, f32[64]{0:T(128)S(1)} %dynamic-update-slice.9, f32[64]{0:T(128)S(1)} %dynamic-update-slice.1, ...), channel_id=15, replica_groups=mesh['gx_0'=4,'gx_1'=2,'gy'=16,'gz'=4] {'gx_1'}, use_global_device_ids=true, to_apply=%add.13 | all-reduce | flops 256 | bytes 2048
  118.6 28.7 %all-reduce.16 = (f32[512]{0:T(512)S(1)}, f32[512]{0:T(512)S(1)}, f32[512]{0:T(512)S(1)}, f32[512]{0:T(512)S(1)}) all-reduce(f32[512]{0:T(512)S(1)} %dynamic-update-slice.14, f32[512]{0:T(512)S(1)} %dynamic-update-slice.10, f32[512]{0:T(512)S(1)} %dynamic-update-slice.2, ...), channel_id=16, replica_groups=mesh['gx_0'=4,'gx_1'=2,'gy'=16,'gz'=4] {'gy'}, use_global_device_ids=true, to_apply=%add.14 | all-reduce | flops 2048 | bytes 16384
  148.6 7.7 %all-reduce.17 = (f32[128]{0:T(128)S(1)}, f32[128]{0:T(128)S(1)}, f32[128]{0:T(128)S(1)}, f32[128]{0:T(128)S(1)}) all-reduce(f32[128]{0:T(128)S(1)} %dynamic-update-slice.15, f32[128]{0:T(128)S(1)} %dynamic-update-slice.11, f32[128]{0:T(128)S(1)} %dynamic-update-slice.3, ...), channel_id=17, replica_groups=mesh['gx_0'=4,'gx_1'=2,'gy'=16,'gz'=4] {'gz'}, use_global_device_ids=true, to_apply=%add.15 | all-reduce | flops 512 | bytes 4096
  156.8 4.1 %multiply_subtract_fusion = f32[32,6,10,130]{3,1,2,0:T(8,128)} fusion(f32[32,6,10,130]{3,1,2,0:T(8,128)} %copy-done.1, f32[32,8,12,132]{3,1,2,0:T(8,128)S(1)} %pad_maximum_fusion, f32[32]{0:T(128)S(1)} %mul.479, f32[32]{0:T(128)S(1)} %get-tuple-element.43), kind=kLoop, calls=%fused_computation.37 | loop fusion | flops 748800 | bytes 2995456 | tf_op jit(solution)/shard_map/sub | solution.py:107
  160.9 4.8 %copy.122 = f32[32,6,10,130]{0,3,2,1:T(8,128)} copy(f32[32,6,10,130]{3,1,2,0:T(8,128)} %multiply_subtract_fusion) | data formatting | bytes 1996800 | tf_op jit(solution)/shard_map/reshape | solution.py:118
  165.8 4.8 %reshape.300 = f32[32,7800]{0,1:T(8,128)} reshape(f32[32,6,10,130]{0,3,2,1:T(8,128)} %copy.122) | data formatting | bytes 1996800 | tf_op jit(solution)/shard_map/reshape | solution.py:118
  170.6 3.0 %gather_fusion.7 = f32[256,32]{1,0:T(8,128)S(1)} fusion(f32[32,7800]{0,1:T(8,128)} %reshape.300, s32[1024]{0:T(1024)} %get-tuple-element.96), kind=kCustom, calls=%fused_computation.5.clone | custom fusion | bytes 66560 | tf_op jit(solution)/shard_map/jit(_take)/gather | solution.py:123
  173.5 3.0 %gather_fusion.6 = f32[256,32]{1,0:T(8,128)S(1)} fusion(f32[32,7800]{0,1:T(8,128)} %reshape.300, s32[1024]{0:T(1024)} %get-tuple-element.97), kind=kCustom, calls=%fused_computation.4.clone | custom fusion | bytes 66560 | tf_op jit(solution)/shard_map/jit(_take)/gather | solution.py:122
  176.5 3.0 %gather_fusion.5 = f32[256,32]{1,0:T(8,128)S(1)} fusion(f32[32,7800]{0,1:T(8,128)} %reshape.300, s32[1024]{0:T(1024)} %get-tuple-element.98), kind=kCustom, calls=%fused_computation.3.clone | custom fusion | bytes 66560 | tf_op jit(solution)/shard_map/jit(_take)/gather | solution.py:123
  179.5 3.0 %gather_fusion.4 = f32[256,32]{1,0:T(8,128)S(1)} fusion(f32[32,7800]{0,1:T(8,128)} %reshape.300, s32[1024]{0:T(1024)} %get-tuple-element.99), kind=kCustom, calls=%fused_computation.2.clone | custom fusion | bytes 66560 | tf_op jit(solution)/shard_map/jit(_take)/gather | solution.py:122
  182.5 3.0 %gather_fusion.3 = f32[256,32]{1,0:T(8,128)S(1)} fusion(f32[32,7800]{0,1:T(8,128)} %reshape.300, s32[1024]{0:T(1024)} %get-tuple-element.100), kind=kCustom, calls=%fused_computation.1.clone | custom fusion | bytes 66560 | tf_op jit(solution)/shard_map/jit(_take)/gather | solution.py:123
  185.5 3.0 %gather_fusion.2 = f32[256,32]{1,0:T(8,128)S(1)} fusion(f32[32,7800]{0,1:T(8,128)} %reshape.300, s32[1024]{0:T(1024)} %get-tuple-element.101), kind=kCustom, calls=%fused_computation.clone | custom fusion | bytes 66560 | tf_op jit(solution)/shard_map/jit(_take)/gather | solution.py:122
  190.3 19.6 %all-to-all-start = ((f32[128,1,192]{2,1,0:T(1,128)}), f32[128,1,192]{2,1,0:T(1,128)S(1)}, u32[]{:S(2)}, u32[]{:S(2)}) async-start(f32[128,1,192]{2,1,0:T(1,128)} %reshape.304), calls=%async_computation | async-start | bytes 262144 | tf_op jit(solution)/shard_map/all_to_all | solution.py:127
  209.9 18.2 %all-to-all-done = f32[128,1,192]{2,1,0:T(1,128)S(1)} async-done(((f32[128,1,192]{2,1,0:T(1,128)}), f32[128,1,192]{2,1,0:T(1,128)S(1)}, u32[]{:S(2)}, u32[]{:S(2)}) %all-to-all-start) | async-done | bytes 98336 | tf_op jit(solution)/shard_map/all_to_all | solution.py:127
  (216 shorter events, 50.5 us)
Async XLA Ops:
  0.6 231.8 %copy-start = (f32[32,128]{1,0:T(8,128)S(1)}, f32[32,128]{1,0:T(8,128)}, u32[]{:S(2)}) copy-start(f32[32,128]{1,0:T(8,128)} %param.13) | copy-start | bytes 49156
  1.4 22.8 %collective-permute-start.6 = (s32[2,8,128]{2,1,0:T(8,128)S(1)}, s32[2,8,128]{2,1,0:T(8,128)S(1)}, u32[]{:S(2)}, u32[]{:S(2)}) collective-permute-start(s32[2,8,128]{2,1,0:T(8,128)S(1)} %get-tuple-element.70), channel_id=1, source_target_pairs={{0,64},{64,128},{128,192},{192,256},{256,320},{320,384},{384,448},... | collective-permute-start | bytes 24584 | tf_op jit(solution)/shard_map/ppermute | solution.py:18
  6.0 18.2 %collective-permute-start.7 = (s32[2,8,128]{2,1,0:T(8,128)S(1)}, s32[2,8,128]{2,1,0:T(8,128)S(1)}, u32[]{:S(2)}, u32[]{:S(2)}) collective-permute-start(s32[2,8,128]{2,1,0:T(8,128)S(1)} %get-tuple-element.71), channel_id=1, source_target_pairs={{64,0},{128,64},{192,128},{256,192},{320,256},{384,320},{448,384},... | collective-permute-start | bytes 24584 | tf_op jit(solution)/shard_map/ppermute | solution.py:21
  12.5 34.1 %collective-permute-start = (f32[32,2,8,128]{3,2,1,0:T(8,128)S(1)}, f32[32,2,8,128]{3,2,1,0:T(8,128)S(1)}, u32[]{:S(2)}, u32[]{:S(2)}) collective-permute-start(f32[32,2,8,128]{3,2,1,0:T(8,128)S(1)} %get-tuple-element.51), channel_id=1, source_target_pairs={{0,64},{64,128},{128,192},{192,256},{256,320},{320,384},{384,448},... | collective-permute-start | bytes 786440 | tf_op jit(solution)/shard_map/ppermute | solution.py:18
  14.4 32.3 %collective-permute-start.1 = (f32[32,2,8,128]{3,2,1,0:T(8,128)S(1)}, f32[32,2,8,128]{3,2,1,0:T(8,128)S(1)}, u32[]{:S(2)}, u32[]{:S(2)}) collective-permute-start(f32[32,2,8,128]{3,2,1,0:T(8,128)S(1)} %get-tuple-element.52), channel_id=1, source_target_pairs={{64,0},{128,64},{192,128},{256,192},{320,256},{384,320},{448,384},... | collective-permute-start | bytes 786440 | tf_op jit(solution)/shard_map/ppermute | solution.py:21
  24.2 5.1 %collective-permute-start.8 = (s32[8,2,128]{2,1,0:T(2,128)S(1)}, s32[8,2,128]{2,1,0:T(2,128)S(1)}, u32[]{:S(2)}, u32[]{:S(2)}) collective-permute-start(s32[8,2,128]{2,1,0:T(2,128)S(1)} %get-tuple-element.68), channel_id=1, source_target_pairs={{0,4},{4,8},{8,12},{12,16},{16,20},{20,24},{24,28},{28,32},{32,36}... | collective-permute-start | bytes 24584 | tf_op jit(solution)/shard_map/ppermute | solution.py:18
  25.5 4.5 %collective-permute-start.9 = (s32[8,2,128]{2,1,0:T(2,128)S(1)}, s32[8,2,128]{2,1,0:T(2,128)S(1)}, u32[]{:S(2)}, u32[]{:S(2)}) collective-permute-start(s32[8,2,128]{2,1,0:T(2,128)S(1)} %get-tuple-element.69), channel_id=1, source_target_pairs={{4,0},{8,4},{12,8},{16,12},{20,16},{24,20},{28,24},{32,28},{36,32}... | collective-permute-start | bytes 24584 | tf_op jit(solution)/shard_map/ppermute | solution.py:21
  28.0 34.2 %copy-start.4 = (f32[32,4,8,128]{3,1,2,0:T(4,128)}, f32[32,4,8,128]{3,1,2,0:T(4,128)S(1)}, u32[]{:S(2)}) copy-start(f32[32,4,8,128]{3,1,2,0:T(4,128)S(1)} %copy.105) | copy-start | bytes 1572868
  30.1 11.1 %collective-permute-start.10 = (s32[8,12,2]{2,1,0:T(8,128)S(1)}, s32[8,12,2]{2,1,0:T(8,128)S(1)}, u32[]{:S(2)}, u32[]{:S(2)}) collective-permute-start(s32[8,12,2]{2,1,0:T(8,128)S(1)} %get-tuple-element.66), channel_id=1, source_target_pairs={{0,1},{1,2},{2,3},{4,5},{5,6},{6,7},{8,9},{9,10},{10,11},{12,13},{... | collective-permute-start | bytes 2312 | tf_op jit(solution)/shard_map/ppermute | solution.py:18
  33.2 7.9 %collective-permute-start.11 = (s32[8,12,2]{2,1,0:T(8,128)S(1)}, s32[8,12,2]{2,1,0:T(8,128)S(1)}, u32[]{:S(2)}, u32[]{:S(2)}) collective-permute-start(s32[8,12,2]{2,1,0:T(8,128)S(1)} %get-tuple-element.67), channel_id=1, source_target_pairs={{1,0},{2,1},{3,2},{5,4},{6,5},{7,6},{9,8},{10,9},{11,10},{13,12},{... | collective-permute-start | bytes 2312 | tf_op jit(solution)/shard_map/ppermute | solution.py:21
  46.9 16.4 %copy-start.7 = (f32[32,2,8,128]{3,1,2,0:T(2,128)}, f32[32,2,8,128]{3,1,2,0:T(2,128)S(1)}, u32[]{:S(2)}) copy-start(f32[32,2,8,128]{3,1,2,0:T(2,128)S(1)} %copy.92) | copy-start | bytes 786436
  47.1 9.5 %collective-permute-start.2 = (f32[32,8,2,128]{3,1,2,0:T(8,128)S(1)}, f32[32,8,2,128]{3,1,2,0:T(8,128)S(1)}, u32[]{:S(2)}, u32[]{:S(2)}) collective-permute-start(f32[32,8,2,128]{3,1,2,0:T(8,128)S(1)} %get-tuple-element.49), channel_id=1, source_target_pairs={{0,4},{4,8},{8,12},{12,16},{16,20},{20,24},{24,28},{28,32},{32,36}... | collective-permute-start | bytes 786440 | tf_op jit(solution)/shard_map/ppermute | solution.py:18
  50.7 11.6 %collective-permute-start.3 = (f32[32,8,2,128]{3,1,2,0:T(8,128)S(1)}, f32[32,8,2,128]{3,1,2,0:T(8,128)S(1)}, u32[]{:S(2)}, u32[]{:S(2)}) collective-permute-start(f32[32,8,2,128]{3,1,2,0:T(8,128)S(1)} %get-tuple-element.50), channel_id=1, source_target_pairs={{4,0},{8,4},{12,8},{16,12},{20,16},{24,20},{28,24},{32,28},{36,32}... | collective-permute-start | bytes 786440 | tf_op jit(solution)/shard_map/ppermute | solution.py:21
  65.0 9.5 %copy-start.25 = (f32[4,8,128]{2,1,0:T(8,128)S(1)}, f32[4,8,128]{2,1,0:T(8,128)}, u32[]{:S(2)}) copy-start(f32[4,8,128]{2,1,0:T(8,128)} %get-tuple-element.58) | copy-start | bytes 49156
  65.0 9.5 %copy-start.24 = (f32[4,8,128]{2,1,0:T(8,128)S(1)}, f32[4,8,128]{2,1,0:T(8,128)}, u32[]{:S(2)}) copy-start(f32[4,8,128]{2,1,0:T(8,128)} %get-tuple-element.53) | copy-start | bytes 49156
  65.0 10.1 %copy-start.23 = (f32[4,8,128]{2,1,0:T(8,128)S(1)}, f32[4,8,128]{2,1,0:T(8,128)}, u32[]{:S(2)}) copy-start(f32[4,8,128]{2,1,0:T(8,128)} %get-tuple-element.54) | copy-start | bytes 49156
  65.0 10.7 %copy-start.22 = (f32[4,8,128]{2,1,0:T(8,128)S(1)}, f32[4,8,128]{2,1,0:T(8,128)}, u32[]{:S(2)}) copy-start(f32[4,8,128]{2,1,0:T(8,128)} %get-tuple-element.55) | copy-start | bytes 49156
  68.1 14.6 %collective-permute-start.5 = (f32[32,8,12,2]{0,1,3,2:T(8,128)S(1)}, f32[32,8,12,2]{0,1,3,2:T(8,128)S(1)}, u32[]{:S(2)}, u32[]{:S(2)}) collective-permute-start(f32[32,8,12,2]{0,1,3,2:T(8,128)S(1)} %copy.94), channel_id=1, source_target_pairs={{1,0},{2,1},{3,2},{5,4},{6,5},{7,6},{9,8},{10,9},{11,10},{13,12},{... | collective-permute-start | bytes 73736 | tf_op jit(solution)/shard_map/ppermute | solution.py:21
  69.4 11.0 %collective-permute-start.4 = (f32[32,8,12,2]{0,1,3,2:T(8,128)S(1)}, f32[32,8,12,2]{0,1,3,2:T(8,128)S(1)}, u32[]{:S(2)}, u32[]{:S(2)}) collective-permute-start(f32[32,8,12,2]{0,1,3,2:T(8,128)S(1)} %copy.93), channel_id=1, source_target_pairs={{0,1},{1,2},{2,3},{4,5},{5,6},{6,7},{8,9},{9,10},{10,11},{12,13},{... | collective-permute-start | bytes 73736 | tf_op jit(solution)/shard_map/ppermute | solution.py:18
  90.1 8.8 %copy-start.6 = (f32[32,4,8,128]{3,2,1,0:T(8,128)S(1)}, f32[32,4,8,128]{3,2,1,0:T(8,128)}, u32[]{:S(2)}) copy-start(f32[32,4,8,128]{3,2,1,0:T(8,128)} %param.8) | copy-start | bytes 1572868
  90.1 8.8 %copy-start.18 = (f32[4,8,128]{2,0,1:T(4,128)S(1)}, f32[4,8,128]{2,0,1:T(4,128)}, u32[]{:S(2)}) copy-start(f32[4,8,128]{2,0,1:T(4,128)} %copy.106) | copy-start | bytes 49156
  90.1 8.8 %copy-start.19 = (f32[4,8,128]{2,0,1:T(4,128)S(1)}, f32[4,8,128]{2,0,1:T(4,128)}, u32[]{:S(2)}) copy-start(f32[4,8,128]{2,0,1:T(4,128)} %copy.109) | copy-start | bytes 49156
  90.1 8.8 %copy-start.20 = (f32[4,8,128]{2,0,1:T(4,128)S(1)}, f32[4,8,128]{2,0,1:T(4,128)}, u32[]{:S(2)}) copy-start(f32[4,8,128]{2,0,1:T(4,128)} %copy.108) | copy-start | bytes 49156
  165.8 22.8 %copy-start.26 = (f32[256]{0:T(256)S(1)}, f32[256]{0:T(256)}, u32[]{:S(2)}) copy-start(f32[256]{0:T(256)} %select_multiply_fusion) | copy-start | bytes 3076
  165.8 22.8 %copy-start.27 = (pred[256]{0:T(512)(128)(4,1)S(1)}, pred[256]{0:T(512)(128)(4,1)}, u32[]{:S(2)}) copy-start(pred[256]{0:T(512)(128)(4,1)} %get-tuple-element.75) | copy-start | bytes 772
  165.8 22.8 %copy-start.28 = (pred[256]{0:T(512)(128)(4,1)S(1)}, pred[256]{0:T(512)(128)(4,1)}, u32[]{:S(2)}) copy-start(pred[256]{0:T(512)(128)(4,1)} %get-tuple-element.76) | copy-start | bytes 772
  165.8 22.8 %copy-start.29 = (pred[256]{0:T(512)(128)(4,1)S(1)}, pred[256]{0:T(512)(128)(4,1)}, u32[]{:S(2)}) copy-start(pred[256]{0:T(512)(128)(4,1)} %get-tuple-element.77) | copy-start | bytes 772
  165.8 22.8 %copy-start.30 = (pred[256]{0:T(512)(128)(4,1)S(1)}, pred[256]{0:T(512)(128)(4,1)}, u32[]{:S(2)}) copy-start(pred[256]{0:T(512)(128)(4,1)} %get-tuple-element.78) | copy-start | bytes 772
  165.8 22.8 %copy-start.31 = (pred[256]{0:T(512)(128)(4,1)S(1)}, pred[256]{0:T(512)(128)(4,1)}, u32[]{:S(2)}) copy-start(pred[256]{0:T(512)(128)(4,1)} %get-tuple-element.79) | copy-start | bytes 772
  165.8 22.8 %copy-start.32 = (pred[256]{0:T(512)(128)(4,1)S(1)}, pred[256]{0:T(512)(128)(4,1)}, u32[]{:S(2)}) copy-start(pred[256]{0:T(512)(128)(4,1)} %get-tuple-element.41) | copy-start | bytes 772
  173.5 36.3 %copy-start.35 = (s32[128]{0:T(128)S(1)}, s32[128]{0:T(128)}, u32[]{:S(2)}) copy-start(s32[128]{0:T(128)} %param.12) | copy-start | bytes 1540
  190.3 37.8 %all-to-all-start = ((f32[128,1,192]{2,1,0:T(1,128)}), f32[128,1,192]{2,1,0:T(1,128)S(1)}, u32[]{:S(2)}, u32[]{:S(2)}) async-start(f32[128,1,192]{2,1,0:T(1,128)} %reshape.304), calls=%async_computation | async-start | bytes 262144 | tf_op jit(solution)/shard_map/all_to_all | solution.py:127
  (17 other events, 74.1 us)
